TPU v7x, 32 devices: a whole 2x2x4 slice. The times are simulated.
32 devices in a mesh: row: 4 (over x, core), col: 8 (over z, y).
Axes of the slice: x: 2, y: 2, z: 4, core: 2. Of those that a mesh axis runs over, the one named last changes fastest.
Arguments:
- homolog_trait_tensor: bfloat16 [192, 8192], P(None, ('row', 'col')), may hold values from -6 to 6
- whitening_multiplier: float32 [64], replicated, may hold values from 0.1 to 1.9
- lefthand_projection: bfloat16 [64, 32], replicated, may hold values from -0.75 to 0.75
- righthand_projection: bfloat16 [64, 32], replicated, may hold values from -0.75 to 0.75
- result_matrix: bfloat16 [1024, 128], replicated, may hold values from -0.75 to 0.75
- result_offset: float32 [128], replicated, may hold values from -3 to 3
- sequence_tallies: int32 [16], replicated, may hold values from 64 to 192
- position_molecule: int32 [128], replicated, may hold values from 0 to 15, never falling along the last dimension, each value on 1 to 16 neighbouring positions
- upstream_adjoint: bfloat16 [128, 128, 128], P('row', 'col'), may hold values from -6 to 6
Outputs:
- couple_update_tensor: bfloat16 [128, 128, 128], P('row', 'col')
- homolog_slope_tensor: float32 [192, 8192], P(None, ('row', 'col'))
- grad_w_out: float32 [1024, 128], replicated
Inputs may be any that keep to these rules, and one draw needn't show every extreme that they name: `position_molecule`: chain numbers never fall along the residues.
All inputs are finite; a program needn't handle non-finite values.
Results may differ from a plain program's by a relative error of at most 0.006.
Values may be sent and summed in bfloat16 or wider, within the bound.
A program may use at most 128 MiB of HBM per device.

v0:
```python
import jax
import jax.numpy as jnp
from jax import lax
from jax.sharding import PartitionSpec as P

EPS_NORM = 1e-05
EPS_COUNT = 0.001


def residue_depths(sequence_tallies, position_molecule, chains):
    table = position_molecule[:, None] == jnp.arange(chains, dtype=jnp.int32)[None, :]
    return jnp.sum(jnp.where(table, sequence_tallies[None, :], 0), axis=1)


def body(
    homolog_trait_tensor,
    whitening_multiplier,
    lefthand_projection,
    righthand_projection,
    result_matrix,
    result_offset,
    sequence_tallies,
    position_molecule,
    upstream_adjoint,
):
    exact_precision = lax.Precision.HIGHEST
    n_row = lax.axis_size("row")
    n_col = lax.axis_size("col")
    row_id = lax.axis_index("row")
    col_id = lax.axis_index("col")
    sequence_number = homolog_trait_tensor.shape[0]
    embedding_size = lefthand_projection.shape[0]
    hidden_features = lefthand_projection.shape[1]
    pair_width = result_matrix.shape[1]
    positions_each_shard = homolog_trait_tensor.shape[1] // embedding_size
    running_total = positions_each_shard * n_row * n_col
    left_extent = running_total // n_row
    right_extent = running_total // n_col
    per_group = n_col // n_row
    column_block = col_id % per_group
    residue_row_depth = residue_depths(
        sequence_tallies, position_molecule, sequence_tallies.shape[0]
    )
    local_depth = lax.dynamic_slice_in_dim(
        residue_row_depth, (row_id * n_col + col_id) * positions_each_shard, positions_each_shard
    )
    local_mask = (
        jnp.arange(sequence_number, dtype=jnp.int32)[:, None] < local_depth[None, :]
    ).astype(jnp.float32)
    operand_tensors = homolog_trait_tensor.astype(jnp.float32).reshape(
        sequence_number, positions_each_shard, embedding_size
    )
    centred = operand_tensors - jnp.mean(operand_tensors, axis=-1, keepdims=True)
    inverse_deviation = lax.rsqrt(jnp.mean(centred * centred, axis=-1, keepdims=True) + EPS_NORM)
    normalized_alignment = centred * inverse_deviation
    scaled_features = normalized_alignment * whitening_multiplier
    left_local = (
        (
            jnp.einsum(
                "yel,lr->yer",
                scaled_features,
                lefthand_projection.astype(jnp.float32),
                precision=exact_precision,
            )
            * local_mask[:, :, None]
        )
        .astype(jnp.bfloat16)
        .reshape(sequence_number, positions_each_shard * hidden_features)
    )
    right_local = (
        (
            jnp.einsum(
                "yel,lr->yer",
                scaled_features,
                righthand_projection.astype(jnp.float32),
                precision=exact_precision,
            )
            * local_mask[:, :, None]
        )
        .astype(jnp.bfloat16)
        .reshape(sequence_number, positions_each_shard * hidden_features)
    )
    left_rows = lax.all_gather(left_local, "col", axis=1, tiled=True)
    right_whole = lax.all_gather(right_local, ("row", "col"), axis=1, tiled=True)
    right_cols = lax.dynamic_slice_in_dim(
        right_whole, col_id * right_extent * hidden_features, right_extent * hidden_features, 1
    )
    depth_rows = lax.dynamic_slice_in_dim(residue_row_depth, row_id * left_extent, left_extent)
    depth_cols = lax.dynamic_slice_in_dim(residue_row_depth, col_id * right_extent, right_extent)
    counts = jnp.minimum(depth_rows[:, None], depth_cols[None, :]).astype(jnp.float32) + EPS_COUNT
    step_rows = 32

    def one_block(carried, block_index):
        coverage_tally_total, right_accumulated_sum = carried
        start = block_index * step_rows
        left_block = lax.dynamic_slice_in_dim(
            left_rows, start * hidden_features, step_rows * hidden_features, 1
        )
        divisor = lax.dynamic_slice_in_dim(counts, start, step_rows, 0)[:, :, None]
        product = lax.dot_general(
            left_block, right_cols, (((0,), (0,)), ((), ())), preferred_element_type=jnp.float32
        )
        outer = (
            product.reshape(step_rows, hidden_features, right_extent, hidden_features)
            .transpose(0, 2, 1, 3)
            .reshape(step_rows, right_extent, hidden_features * hidden_features)
        )
        outer = (outer / divisor).astype(jnp.bfloat16)
        flat = outer.reshape(step_rows * right_extent, hidden_features * hidden_features)
        update = (
            jnp.dot(flat, result_matrix, preferred_element_type=jnp.float32) + result_offset
        ).astype(jnp.bfloat16)
        update = update.reshape(step_rows, right_extent, pair_width)
        incoming = lax.dynamic_slice_in_dim(upstream_adjoint, start, step_rows, 0).reshape(
            step_rows * right_extent, pair_width
        )
        coverage_tally_total = coverage_tally_total + jnp.dot(
            flat.T, incoming, preferred_element_type=jnp.float32
        )
        grad_outer = jnp.dot(incoming, result_matrix.T, preferred_element_type=jnp.float32).reshape(
            step_rows, right_extent, hidden_features * hidden_features
        )
        grad_outer = (grad_outer / divisor).astype(jnp.bfloat16)
        grad_matrix = (
            grad_outer.reshape(step_rows, right_extent, hidden_features, hidden_features)
            .transpose(0, 2, 1, 3)
            .reshape(step_rows * hidden_features, right_extent * hidden_features)
        )
        left_grad = lax.dot_general(
            right_cols, grad_matrix, (((1,), (1,)), ((), ())), preferred_element_type=jnp.float32
        )
        right_accumulated_sum = right_accumulated_sum + jnp.dot(
            left_block, grad_matrix, preferred_element_type=jnp.float32
        )
        return ((coverage_tally_total, right_accumulated_sum), (update, left_grad))

    initial_state = (
        jnp.zeros((hidden_features * hidden_features, pair_width), jnp.float32),
        jnp.zeros((sequence_number, right_extent * hidden_features), jnp.float32),
    )
    (coverage_tally_total, right_accumulated_sum), (updates, left_gradient_rows) = lax.scan(
        one_block, initial_state, jnp.arange(left_extent // step_rows, dtype=jnp.int32)
    )
    couple_update_tensor = updates.reshape(left_extent, right_extent, pair_width)
    left_partial_sum = left_gradient_rows.transpose(1, 0, 2).reshape(
        sequence_number, left_extent * hidden_features
    )
    right_summed = lax.psum(right_accumulated_sum, "row")
    owner_flag = (row_id == col_id // per_group).astype(jnp.float32)
    placed = lax.dynamic_update_slice_in_dim(
        jnp.zeros((sequence_number, left_extent * hidden_features), jnp.float32),
        right_summed * owner_flag,
        column_block * right_extent * hidden_features,
        1,
    )
    left_portion, right_portion = (
        lax.psum_scatter(left_partial_sum, "col", scatter_dimension=1, tiled=True),
        lax.psum_scatter(placed, "col", scatter_dimension=1, tiled=True),
    )
    left_grand_total = (
        left_portion.reshape(sequence_number, positions_each_shard, hidden_features)
        * local_mask[:, :, None]
    )
    right_grand_total = (
        right_portion.reshape(sequence_number, positions_each_shard, hidden_features)
        * local_mask[:, :, None]
    )
    grad_scaled = jnp.einsum(
        "snh,ch->snc",
        left_grand_total,
        lefthand_projection.astype(jnp.float32),
        precision=exact_precision,
    )
    grad_scaled = grad_scaled + jnp.einsum(
        "snh,ch->snc",
        right_grand_total,
        righthand_projection.astype(jnp.float32),
        precision=exact_precision,
    )
    normed_gradient = grad_scaled * whitening_multiplier
    homolog_slope_tensor = inverse_deviation * (
        normed_gradient
        - jnp.mean(normed_gradient, axis=-1, keepdims=True)
        - normalized_alignment
        * jnp.mean(normed_gradient * normalized_alignment, axis=-1, keepdims=True)
    )
    mask_weight_total = lax.psum(coverage_tally_total, ("row", "col"))
    return (
        couple_update_tensor,
        homolog_slope_tensor.reshape(sequence_number, positions_each_shard * embedding_size),
        mask_weight_total / running_total,
    )


def solution(mesh):
    in_specs = (P(None, ("row", "col")), P(), P(), P(), P(), P(), P(), P(), P("row", "col", None))
    out_specs = (P("row", "col", None), P(None, ("row", "col")), P())
    return jax.shard_map(body, mesh=mesh, in_specs=in_specs, out_specs=out_specs, check_vma=False)
```

profile of v0, /device:TPU:1, one launch (start us, length us, event | category | flops | bytes accessed | tf_op | source)
XLA Modules:
  0.0 244.8 jit_solution(8979142956524414565)
XLA Ops:
  8.0 0.0 copy-start
  8.0 0.0 all-gather.2.cloned.1.call-start
  8.1 0.8 select_reduce_fusion
  8.9 0.1 dynamic_slice.21
  8.9 0.1 fusion.29
  9.0 1.0 copy.27
  10.1 1.7 fusion.3
  11.8 0.0 all-gather.2.cloned.1.call-update
  11.8 0.0 all-reduce.3.cloned.1.call-start
  11.9 0.1 dynamic_slice.24
  11.9 0.1 dynamic_slice.23
  12.0 0.1 convert_add_fusion
  12.1 0.0 copy-done
  12.1 1.3 divide_convert_fusion.1
  13.4 4.4 %reshape.145 = bf16[32,16,32,32]{3,2,1,0:T(8,128)(2,1)} reshape(bf16[32,16,1024]{2,1,0:T(8,128)(2,1)S(1)} %divide_convert_fusion.1) | data formatting | bytes 2097152 | tf_op jit(solution)/shard_map/while/body/eval_jaxpr/reshape | solution.py:125
  17.8 6.1 %copy.36 = bf16[32,16,32,32]{3,1,2,0:T(8,128)(2,1)} copy(bf16[32,16,32,32]{3,2,1,0:T(8,128)(2,1)} %reshape.145) | data formatting | bytes 2097152 | tf_op jit(solution)/shard_map/while/body/eval_jaxpr/reshape | solution.py:125
  23.9 0.0 copy-start.3
  23.9 0.0 copy-start.4
  23.9 6.0 %reshape.146 = bf16[1024,512]{1,0:T(8,128)(2,1)S(1)} reshape(bf16[32,32,16,32]{3,2,1,0:T(8,128)(2,1)} %bitcast.63) | data formatting | bytes 2097152 | tf_op jit(solution)/shard_map/while/body/eval_jaxpr/reshape | solution.py:127
  29.9 0.0 copy-done.3
  29.9 0.0 copy-done.4
  29.9 0.3 fusion.2
  30.2 26.9 %all_gather.6 = bf16[192,1024]{0,1:T(8,128)(2,1)S(1)} all-gather(bf16[192,128]{0,1:T(8,128)(2,1)S(1)} %bitcast.66), channel_id=1, replica_groups=mesh['row'=4,'col'=8] {'col'}, dimensions={1}, use_global_device_ids=true | all-gather | bytes 442368 | tf_op jit(solution)/shard_map/all_gather | solution.py:83
  57.1 1.2 fusion.33
  58.3 0.0 all-reduce.3.cloned.1.call-update
  58.3 0.2 all-reduce.5.cloned.1.call-start
  58.5 13.4 %all-gather.2.cloned.1.call-done = bf16[192,4096]{0,1:T(8,128)(2,1)} async-done(((bf16[192,128]{0,1:T(8,128)(2,1)}), bf16[192,4096]{0,1:T(8,128)(2,1)}) %all-gather.2.cloned.1.call-update) | async-done | bytes 1572880 | tf_op jit(solution)/shard_map/all_gather | solution.py:84
  71.9 2.8 %fusion.10 = f32[1024,512]{1,0:T(8,128)} fusion(bf16[192,1024]{0,1:T(8,128)(2,1)S(1)} %all_gather.6, bf16[192,4096]{0,1:T(8,128)(2,1)} %all-gather.2.cloned.1.call-done, s32[]{:T(128)S(6)} %select_n.37), kind=kOutput, calls=%fused_computation.26 | convolution fusion | flops 201326592 | bytes 2752516 | tf_op jit(solution)/shard_map/while/body/eval_jaxpr/dot_general | solution.py:100
  74.7 6.2 %reshape.142 = f32[32,32,16,32]{3,2,1,0:T(8,128)} reshape(f32[1024,512]{1,0:T(8,128)} %fusion.10) | data formatting | bytes 4194304 | tf_op jit(solution)/shard_map/while/body/eval_jaxpr/reshape | solution.py:104
  80.9 10.1 %copy.35 = f32[32,32,16,32]{3,1,2,0:T(8,128)} copy(f32[32,32,16,32]{3,2,1,0:T(8,128)} %reshape.142) | data formatting | bytes 4194304 | tf_op jit(solution)/shard_map/while/body/eval_jaxpr/reshape | solution.py:104
  90.9 0.0 copy-start.5
  90.9 7.7 %reshape.150 = f32[32,16,1024]{2,1,0:T(8,128)} reshape(f32[32,16,32,32]{3,2,1,0:T(8,128)} %bitcast.61) | data formatting | bytes 4194304 | tf_op jit(solution)/shard_map/while/body/eval_jaxpr/reshape | solution.py:106
  98.7 0.0 copy-done.5
  98.7 3.0 %convolution_bitcast_fusion = f32[1024,128]{1,0:T(8,128)} fusion(bf16[32,16,128]{2,1,0:T(8,128)(2,1)S(1)} %copy-done.5, f32[32,16,1024]{2,1,0:T(8,128)} %reshape.150, f32[32,16]{1,0:T(8,128)S(1)} %convert_add_fusion), kind=kOutput, calls=%fused_computation.5 | convolution fusion | flops 135266304 | bytes 2754560 | tf_op jit(solution)/shard_map/while/body/eval_jaxpr/dot_general | solution.py:117
  101.6 0.0 all-reduce.5.cloned.1.call-update
  101.7 0.0 reduce-scatter.3.cloned.1.call-start
  101.7 2.4 fusion.8
  104.1 0.0 reduce-scatter.3.cloned.1.call-update
  104.1 0.0 reduce-scatter.5.cloned.1.call-start
  104.2 0.0 all-reduce.3.cloned.1.call-done
  104.2 1.0 broadcast_multiply_fusion.1
  105.2 0.2 copy.31
  105.4 0.1 broadcast_in_dim.22
  105.6 0.0 copy-start.1
  105.6 1.1 copy-done.1
  106.6 0.0 reduce-scatter.5.cloned.1.call-update
  106.7 0.1 min.29
  106.8 0.1 min.26
  106.8 0.1 min.27
  106.9 0.0 copy-start.6
  106.9 6.7 %reshape.143 = f32[512,1024]{1,0:T(8,128)S(1)} reshape(f32[32,16,32,32]{3,2,1,0:T(8,128)} %bitcast.62) | data formatting | bytes 4194304 | tf_op jit(solution)/shard_map/while/body/eval_jaxpr/reshape | solution.py:106
  113.6 0.0 copy-done.6
  113.6 0.0 copy-start.2
  113.6 1.1 fusion.1
  114.8 117.5 %all-reduce.5.cloned.1.call-done = f32[1024,128]{1,0:T(8,128)} async-done(((f32[1024,128]{1,0:T(8,128)}), f32[1024,128]{1,0:T(8,128)}) %all-reduce.5.cloned.1.call-update) | async-done | bytes 524304 | tf_op jit(solution)/shard_map/psum | solution.py:187
  232.3 1.9 broadcast_multiply_fusion
  234.2 0.0 reduce-scatter.3.cloned.1.call-done
  234.2 1.0 copy.30
  235.2 0.3 fusion.15
  235.5 0.0 reduce-scatter.5.cloned.1.call-done
  235.5 0.0 copy-done.2
  235.5 1.3 fusion.32
  236.8 0.1 subtract_multiply_fusion
  236.9 0.8 copy.32
  (8 shorter events, 0.1 us)
Async XLA Ops:
  8.0 4.1 %copy-start = (bf16[1024,128]{1,0:T(8,128)(2,1)S(1)}, bf16[1024,128]{1,0:T(8,128)(2,1)}, u32[]{:S(2)}) copy-start(bf16[1024,128]{1,0:T(8,128)(2,1)} %param.13) | copy-start | bytes 786436
  8.0 63.9 %all-gather.2.cloned.1.call-start = ((), (), s32[]{:S(2)}) async-start(), calls=%async_computation.2 | async-start | bytes 2162688 | tf_op jit(solution)/shard_map/all_gather | solution.py:84
  11.8 92.4 %all-reduce.3.cloned.1.call-start = ((), (), s32[]{:S(2)}) async-start(), calls=%async_computation.4 | async-start | bytes 786432 | tf_op jit(solution)/shard_map/psum | solution.py:148
  23.9 6.0 %copy-start.3 = (bf16[64,32]{0,1:T(8,128)(2,1)S(1)}, bf16[64,32]{0,1:T(8,128)(2,1)}, u32[]{:S(2)}) copy-start(bf16[64,32]{0,1:T(8,128)(2,1)} %param.11) | copy-start | bytes 12292
  23.9 6.0 %copy-start.4 = (f32[64]{0:T(128)S(1)}, f32[64]{0:T(128)}, u32[]{:S(2)}) copy-start(f32[64]{0:T(128)} %param.10) | copy-start | bytes 772
  58.3 174.0 %all-reduce.5.cloned.1.call-start = ((), (), s32[]{:S(2)}) async-start(), calls=%async_computation.6 | async-start | bytes 1048576 | tf_op jit(solution)/shard_map/psum | solution.py:187
  90.9 7.8 %copy-start.5 = (bf16[32,16,128]{2,1,0:T(8,128)(2,1)S(1)}, bf16[32,16,128]{2,1,0:T(8,128)(2,1)}, u32[]{:S(2)}) copy-start(bf16[32,16,128]{2,1,0:T(8,128)(2,1)} %param.17) | copy-start | bytes 393220
  101.7 132.5 %reduce-scatter.3.cloned.1.call-start = ((), (), s32[]{:S(2)}) async-start(), calls=%async_computation.3 | async-start | bytes 884736 | tf_op jit(solution)/shard_map/reduce_scatter | solution.py:157
  104.1 131.4 %reduce-scatter.5.cloned.1.call-start = ((), (), s32[]{:S(2)}) async-start(), calls=%async_computation.5 | async-start | bytes 1179648 | tf_op jit(solution)/shard_map/reduce_scatter | solution.py:158
  105.6 1.1 copy-start.1
  106.9 6.7 %copy-start.6 = (f32[128]{0:T(128)S(1)}, f32[128]{0:T(128)}, u32[]{:S(2)}) copy-start(f32[128]{0:T(128)} %param.14) | copy-start | bytes 1540
  113.6 121.9 %copy-start.2 = (bf16[64,32]{0,1:T(8,128)(2,1)S(1)}, bf16[64,32]{0,1:T(8,128)(2,1)}, u32[]{:S(2)}) copy-start(bf16[64,32]{0,1:T(8,128)(2,1)} %param.12) | copy-start | bytes 12292
Sparse Core Ops, SparseCore 0:
  12.4 59.4 all-gather.1
  105.8 60.6 reduce-scatter.2
  169.9 62.9 reduce-scatter.4
Sparse Core Ops, SparseCore 1:
  58.4 38.0 all-reduce.2
  102.2 130.1 all-reduce.4
where the time goes:
time: 248 us; the launch traced here: 245 us
  waiting for transfers between devices  131 us (53%)
  local copies, waits for them, and re-layouts  51.8 us (21%)
  blocking collectives  26.9 us (11%)
  between operations  15.5 us (6%)
  matrix products  15.3 us (6%)
  other arithmetic  4 us (2%)
    psum x1, waiting for transfers between devices, body(): mask_weight_total = lax.psum(coverage_tally_total, ('row', 'col'))  118 us
    all_gather x1, blocking collectives, body(): left_rows = lax.all_gather(left_local, 'col', axis=1, tiled=True)  26.9 us
    reshape x2, local copies, waits for them, and re-layouts, one_block(): product.reshape(step_rows, hidden_features, right_extent, hidden_features)  16.2 us
    reshape x2, local copies, waits for them, and re-layouts, one_block(): outer = product.reshape(step_rows, hidden_features, right_extent, hidden_...  14.4 us
    all_gather x1, waiting for transfers between devices, body(): lax.all_gather(right_local, ('row', 'col'), axis=1, tiled=True)  13.4 us
    reshape x2, local copies, waits for them, and re-layouts, one_block(): grad_outer.reshape(step_rows, right_extent, hidden_features, hidden_featu...  10.5 us
    reshape x1, local copies, waits for them, and re-layouts, one_block(): grad_matrix = grad_outer.reshape(step_rows, right_extent, hidden_features...  5.96 us
  transfers between devices with their start and end apart: 5, of which 2 were waited for; matrix products, arithmetic and copies ran while one was open for 26% of the time, Pallas kernels for 0%

commit v1 on v0

v1 whole, which is shorter than its diff:
```python
import functools

import jax
import jax.numpy as jnp
from jax import lax
from jax.experimental import pallas as pl
from jax.experimental.pallas import tpu as pltpu
from jax.sharding import PartitionSpec as P

EPS_NORM = 1e-05
EPS_COUNT = 0.001
LANES = 128
BLOCK = 32

f32 = jnp.float32
bf16 = jnp.bfloat16


def dotf(a, b, dims):
    return lax.dot_general(a, b, (dims, ((), ())), preferred_element_type=f32)


def dot_exact(a, b, dims):
    first = a.astype(bf16)
    rest = a - first.astype(f32)
    second = rest.astype(bf16)
    third = (rest - second.astype(f32)).astype(bf16)
    return dotf(third, b, dims) + dotf(second, b, dims) + dotf(first, b, dims)


NN = ((1,), (0,))
NT = ((1,), (1,))
TN = ((0,), (0,))


def kernel(
    n_row, n_col, hidden, embed,
    x_ref, gain_ref, proj_ref, w_ref, offset_ref, depth_ref, recip_ref, adj_ref,
    upd_ref, slope_ref, gw_out_ref,
    normed_ref, inv_ref, lsend_ref, rsend_ref, lall_ref, rall_ref, prod_ref, flat_ref,
    adjf_ref, adjt_ref, updf_ref, gacc_ref, gwsend_ref, w1_ref, w2_ref, w3_ref,
    go_ref, gm_ref, glsend_ref, gracc_ref, grsend_ref, gl_ref, gr_ref,
    ls_sem, lr_sem, rs_sem, rr_sem, gls_sem, glr_sem, grs_sem, grr_sem,
    w1s_sem, w1r_sem, w2s_sem, w2r_sem, w3s_sem, w3r_sem,
):
    r = lax.axis_index("row")
    c = lax.axis_index("col")
    group = n_col // n_row
    depth_s = x_ref.shape[0]
    width = lsend_ref.shape[1]
    per_vreg = LANES // hidden
    left_extent = recip_ref.shape[0]
    right_extent = recip_ref.shape[1] // hidden
    chunks = left_extent // BLOCK
    channels = hidden * hidden
    total = n_row * n_col * (x_ref.shape[1] // embed)

    to_col = r * group + c // n_row
    to_slot = lax.rem(c, n_row)
    own_row = c // group
    own_col = lax.rem(c, group) * n_row
    loops_back = to_col == c

    barrier = pltpu.get_barrier_semaphore()

    def greet(row, col):
        pl.semaphore_signal(
            barrier, inc=1, device_id=(row, col), device_id_type=pl.DeviceIdType.MESH
        )

    for o in range(1, n_col):
        greet(r, lax.rem(c + o, n_col))
    for o in range(1, n_row):
        greet(lax.rem(r + o, n_row), c)
    for k in range(n_row):
        self_target = loops_back & (r == k)
        self_owner = (own_row == r) & (own_col + k == c)

        @pl.when(jnp.logical_not(self_target))
        def _():
            greet(k, to_col)

        @pl.when(jnp.logical_not(self_owner))
        def _():
            greet(own_row, own_col + k)

    def remote(src, dst, send_sem, recv_sem, row, col):
        return pltpu.make_async_remote_copy(
            src_ref=src, dst_ref=dst, send_sem=send_sem, recv_sem=recv_sem,
            device_id=(row, col), device_id_type=pl.DeviceIdType.MESH,
        )

    full = x_ref.shape[1]
    same = (
        lax.broadcasted_iota(jnp.int32, (full, full), 0) // embed
        == lax.broadcasted_iota(jnp.int32, (full, full), 1) // embed
    )
    averager = jnp.where(same, 1.0 / embed, 0.0).astype(bf16)
    x = x_ref[...]
    centred = x.astype(f32) - dotf(x, averager, NN)
    inv = lax.rsqrt(dot_exact(centred * centred, averager, NN) + EPS_NORM)
    normed = centred * inv
    normed_ref[...] = normed
    inv_ref[...] = inv
    gain = gain_ref[...]
    keep = (
        lax.broadcasted_iota(jnp.int32, (depth_s, width), 0) < depth_ref[...]
    ).astype(f32)
    both = dot_exact(normed * gain, proj_ref[...], NN)
    left = (both[:, :width] * keep).astype(bf16)
    right = (both[:, width:] * keep).astype(bf16)
    rsend_ref[...] = right
    lsend_ref[...] = left

    def panel(ref, index):
        return ref.at[:, pl.ds(pl.multiple_of(index * width, LANES), width)]

    pl.semaphore_wait(
        barrier, n_col - 1 + n_row - 1 + 2 * n_row - 2 * loops_back.astype(jnp.int32)
    )

    def left_copy(o):
        return remote(
            lsend_ref, panel(lall_ref, c), ls_sem.at[o], lr_sem.at[c],
            r, lax.rem(c + o, n_col),
        )

    def right_copy(k):
        return remote(
            rsend_ref, panel(rall_ref, to_slot), rs_sem.at[k], rr_sem.at[to_slot], k, to_col
        )

    for k in range(n_row):
        self_target = loops_back & (r == k)

        @pl.when(jnp.logical_not(self_target))
        def _():
            right_copy(k).start()

    for o in range(1, n_col):
        left_copy(o).start()

    @pl.when(loops_back & (r == own_row))
    def _():
        panel(rall_ref, to_slot)[...] = rsend_ref[...]

    panel(lall_ref, c)[...] = left

    rows = BLOCK * right_extent
    for b in range(chunks):
        adjf_ref[...] = adj_ref[b * rows : (b + 1) * rows, :].astype(f32)
        for j in range(right_extent):
            adjt_ref[b * rows + j * BLOCK : b * rows + (j + 1) * BLOCK, :] = adjf_ref[
                pl.ds(j, BLOCK, stride=right_extent), :
            ].astype(bf16)

    for k in range(n_row):
        self_owner = (own_row == r) & (own_col + k == c)

        @pl.when(jnp.logical_not(self_owner))
        def _():
            remote(
                rsend_ref, panel(rall_ref, k), rs_sem.at[k], rr_sem.at[k], own_row, own_col + k
            ).wait_recv()

    for o in range(1, n_col):
        source = lax.rem(c + o, n_col)
        remote(
            lsend_ref, panel(lall_ref, source), ls_sem.at[o], lr_sem.at[source], r, source
        ).wait_recv()

    lane_part = lax.broadcasted_iota(jnp.int32, (BLOCK, LANES), 1) // hidden
    groups_j = right_extent // per_vreg
    groups_h = hidden // per_vreg

    def regroup(tiles, own):
        merged = None
        for t in range(per_vreg):
            shift = ((t - own) * hidden) % LANES
            moved = pltpu.roll(tiles[t], shift, 1) if shift else tiles[t]
            merged = moved if merged is None else jnp.where(lane_part == t, moved, merged)
        return merged

    span = BLOCK * hidden
    gacc_ref[...] = jnp.zeros_like(gacc_ref)

    def forward(b, _):
        start = pl.multiple_of(b * rows, rows)
        recip = recip_ref[pl.ds(pl.multiple_of(b * BLOCK, BLOCK), BLOCK), :]
        left_block = lall_ref[:, pl.ds(pl.multiple_of(b * span, span), span)]
        product = dotf(left_block, rall_ref[...], TN)
        for jq in range(groups_j):
            prod_ref[jq] = product[:, jq * LANES : (jq + 1) * LANES]
        for hq in range(groups_h):
            for jq in range(groups_j):
                scale = recip[:, jq * LANES : (jq + 1) * LANES]
                tiles = [
                    prod_ref[jq, pl.ds(hq * per_vreg + t, BLOCK, stride=hidden), :] * scale
                    for t in range(per_vreg)
                ]
                for jj in range(per_vreg):
                    j = jq * per_vreg + jj
                    flat_ref[
                        j * BLOCK : (j + 1) * BLOCK, hq * LANES : (hq + 1) * LANES
                    ] = regroup(tiles, jj).astype(bf16)
        flat = flat_ref[...]
        incoming = adjt_ref[pl.ds(start, rows), :]
        gacc_ref[...] += dotf(incoming, flat, TN)
        update = dotf(flat, w_ref[...], NN) + offset_ref[...]
        for j in range(right_extent):
            updf_ref[pl.ds(j, BLOCK, stride=right_extent), :] = update[
                j * BLOCK : (j + 1) * BLOCK, :
            ]
        upd_ref[pl.ds(start, rows), :] = updf_ref[...].astype(bf16)
        return 0

    lax.fori_loop(0, chunks, forward, 0)

    piece = channels // n_col
    gwsend_ref[...] = gacc_ref[...].T.astype(bf16)

    def w_rows(ref, index):
        return ref.at[pl.ds(pl.multiple_of(index * piece, piece), piece), :]

    def w1_copy(o):
        target = lax.rem(c + o, n_col)
        return remote(
            w_rows(gwsend_ref, target), w1_ref.at[c], w1s_sem.at[o], w1r_sem.at[c], r, target
        )

    for o in range(1, n_col):
        w1_copy(o).start()
    w1_ref[c] = w_rows(gwsend_ref, c)[...]

    gracc_ref[...] = jnp.zeros_like(gracc_ref)

    def backward(b, _):
        start = pl.multiple_of(b * rows, rows)
        recip = recip_ref[pl.ds(pl.multiple_of(b * BLOCK, BLOCK), BLOCK), :]
        left_block = lall_ref[:, pl.ds(pl.multiple_of(b * span, span), span)]
        go_ref[...] = dotf(adjt_ref[pl.ds(start, rows), :], w_ref[...], NT)
        for hq in range(groups_h):
            for jq in range(groups_j):
                scale = recip[:, jq * LANES : (jq + 1) * LANES]
                tiles = [
                    go_ref[
                        (jq * per_vreg + t) * BLOCK : (jq * per_vreg + t + 1) * BLOCK,
                        hq * LANES : (hq + 1) * LANES,
                    ]
                    for t in range(per_vreg)
                ]
                for hh in range(per_vreg):
                    gm_ref[jq, pl.ds(hq * per_vreg + hh, BLOCK, stride=hidden), :] = (
                        regroup(tiles, hh) * scale
                    )
        grad = jnp.concatenate([gm_ref[jq].astype(bf16) for jq in range(groups_j)], axis=1)
        glsend_ref[:, pl.ds(pl.multiple_of(b * span, span), span)] = dotf(
            rall_ref[...], grad, NT
        ).astype(bf16)
        gracc_ref[...] += dotf(left_block, grad, NN)
        return 0

    lax.fori_loop(0, chunks, backward, 0)

    def gl_copy(o):
        target = lax.rem(c + o, n_col)
        return remote(
            panel(glsend_ref, target), gl_ref.at[c], gls_sem.at[o], glr_sem.at[c], r, target
        )

    def gr_copy(k):
        return remote(
            panel(grsend_ref, k), gr_ref.at[r], grs_sem.at[k], grr_sem.at[r],
            own_row, own_col + k,
        )

    for o in range(1, n_col):
        gl_copy(o).start()
    grsend_ref[...] = gracc_ref[...].astype(bf16)
    gl_ref[c] = panel(glsend_ref, c)[...]
    for k in range(n_row):
        self_owner = (own_row == r) & (own_col + k == c)

        @pl.when(jnp.logical_not(self_owner))
        def _():
            gr_copy(k).start()

        @pl.when(self_owner)
        def _():
            gr_ref[r] = panel(grsend_ref, k)[...]

    for o in range(1, n_col):
        source = lax.rem(c + o, n_col)
        remote(
            w_rows(gwsend_ref, source), w1_ref.at[source], w1s_sem.at[o], w1r_sem.at[source],
            r, source,
        ).wait_recv()
    partial = w1_ref[0].astype(f32)
    for d in range(1, n_col):
        partial = partial + w1_ref[d].astype(f32)
    w2_ref[r] = partial.astype(bf16)

    def w2_copy(o):
        return remote(
            w2_ref.at[r], w2_ref.at[r], w2s_sem.at[o], w2r_sem.at[r], lax.rem(r + o, n_row), c
        )

    for o in range(1, n_row):
        w2_copy(o).start()

    for o in range(1, n_row):
        source = lax.rem(r + o, n_row)
        remote(
            w2_ref.at[source], w2_ref.at[source], w2s_sem.at[o], w2r_sem.at[source], source, c
        ).wait_recv()
    whole = w2_ref[0].astype(f32)
    for d in range(1, n_row):
        whole = whole + w2_ref[d].astype(f32)
    w_rows(w3_ref, c)[...] = (whole * (1.0 / total)).astype(bf16)

    def w3_copy(o):
        return remote(
            w_rows(w3_ref, c), w_rows(w3_ref, c), w3s_sem.at[o], w3r_sem.at[c],
            r, lax.rem(c + o, n_col),
        )

    for o in range(1, n_col):
        w3_copy(o).start()

    for o in range(1, n_col):
        source = lax.rem(c + o, n_col)
        remote(
            panel(glsend_ref, source), gl_ref.at[source], gls_sem.at[o], glr_sem.at[source],
            r, source,
        ).wait_recv()
    for k in range(n_row):
        self_target = loops_back & (r == k)

        @pl.when(jnp.logical_not(self_target))
        def _():
            remote(
                panel(grsend_ref, 0), gr_ref.at[k], grs_sem.at[k], grr_sem.at[k], k, to_col
            ).wait_recv()

    grad_left = gl_ref[0].astype(f32)
    for d in range(1, n_col):
        grad_left = grad_left + gl_ref[d].astype(f32)
    grad_right = gr_ref[0].astype(f32)
    for d in range(1, n_row):
        grad_right = grad_right + gr_ref[d].astype(f32)
    keep = (
        lax.broadcasted_iota(jnp.int32, (depth_s, width), 0) < depth_ref[...]
    ).astype(f32)
    sides = jnp.concatenate([grad_left * keep, grad_right * keep], axis=1)
    grad_norm = dot_exact(sides, proj_ref[...], NT) * gain_ref[...]
    normed = normed_ref[...]
    slope_ref[...] = inv_ref[...] * (
        grad_norm
        - dot_exact(grad_norm, averager, NN)
        - normed * dot_exact(grad_norm * normed, averager, NN)
    )

    for o in range(1, n_col):
        source = lax.rem(c + o, n_col)
        remote(
            w_rows(w3_ref, source), w_rows(w3_ref, source), w3s_sem.at[o], w3r_sem.at[source],
            r, source,
        ).wait_recv()
    gw_out_ref[...] = w3_ref[...].astype(f32)

    for o in range(1, n_col):
        left_copy(o).wait_send()
        w1_copy(o).wait_send()
        gl_copy(o).wait_send()
        w3_copy(o).wait_send()
    for o in range(1, n_row):
        w2_copy(o).wait_send()
    for k in range(n_row):
        self_target = loops_back & (r == k)
        self_owner = (own_row == r) & (own_col + k == c)

        @pl.when(jnp.logical_not(self_target))
        def _():
            right_copy(k).wait_send()

        @pl.when(jnp.logical_not(self_owner))
        def _():
            gr_copy(k).wait_send()


def body(
    homolog_trait_tensor,
    whitening_multiplier,
    lefthand_projection,
    righthand_projection,
    result_matrix,
    result_offset,
    sequence_tallies,
    position_molecule,
    upstream_adjoint,
):
    n_row = lax.axis_size("row")
    n_col = lax.axis_size("col")
    row_id = lax.axis_index("row")
    col_id = lax.axis_index("col")
    depth_s, full = homolog_trait_tensor.shape
    embed, hidden = lefthand_projection.shape
    pair_width = result_matrix.shape[1]
    local = full // embed
    total = local * n_row * n_col
    left_extent = total // n_row
    right_extent = total // n_col
    width = local * hidden
    channels = hidden * hidden
    rows = BLOCK * right_extent
    span = BLOCK * hidden

    table = position_molecule[:, None] == jnp.arange(sequence_tallies.shape[0])[None, :]
    depth = jnp.sum(jnp.where(table, sequence_tallies[None, :], 0), axis=1)
    depth_local = lax.dynamic_slice_in_dim(depth, (row_id * n_col + col_id) * local, local)
    depth_rows = lax.dynamic_slice_in_dim(depth, row_id * left_extent, left_extent)
    depth_cols = lax.dynamic_slice_in_dim(depth, col_id * right_extent, right_extent)
    depth_lanes = jnp.repeat(depth_local, hidden)[None, :]
    recip = 1.0 / (
        jnp.minimum(depth_rows[:, None], jnp.repeat(depth_cols, hidden)[None, :]).astype(f32)
        + EPS_COUNT
    )
    eye = jnp.eye(local, dtype=bf16)
    projections = jnp.concatenate(
        [jnp.kron(eye, lefthand_projection), jnp.kron(eye, righthand_projection)], axis=1
    )
    gain = jnp.tile(whitening_multiplier, local)[None, :]

    vmem = pl.BlockSpec(memory_space=pltpu.VMEM)
    dma = pltpu.SemaphoreType.DMA
    update, slope, grad_w = pl.pallas_call(
        functools.partial(kernel, n_row, n_col, hidden, embed),
        out_shape=(
            jax.ShapeDtypeStruct((left_extent * right_extent, pair_width), bf16),
            jax.ShapeDtypeStruct((depth_s, full), f32),
            jax.ShapeDtypeStruct((channels, pair_width), f32),
        ),
        in_specs=[vmem] * 8,
        out_specs=(vmem,) * 3,
        scratch_shapes=[
            pltpu.VMEM((depth_s, full), f32),
            pltpu.VMEM((depth_s, full), f32),
            pltpu.VMEM((depth_s, width), bf16),
            pltpu.VMEM((depth_s, width), bf16),
            pltpu.VMEM((depth_s, left_extent * hidden), bf16),
            pltpu.VMEM((depth_s, right_extent * hidden), bf16),
            pltpu.VMEM((right_extent * hidden // LANES, span, LANES), f32),
            pltpu.VMEM((rows, channels), bf16),
            pltpu.VMEM((rows, pair_width), f32),
            pltpu.VMEM((left_extent * right_extent, pair_width), bf16),
            pltpu.VMEM((rows, pair_width), f32),
            pltpu.VMEM((pair_width, channels), f32),
            pltpu.VMEM((channels, pair_width), bf16),
            pltpu.VMEM((n_col, channels // n_col, pair_width), bf16),
            pltpu.VMEM((n_row, channels // n_col, pair_width), bf16),
            pltpu.VMEM((channels, pair_width), bf16),
            pltpu.VMEM((rows, channels), f32),
            pltpu.VMEM((right_extent * hidden // LANES, span, LANES), f32),
            pltpu.VMEM((depth_s, left_extent * hidden), bf16),
            pltpu.VMEM((depth_s, right_extent * hidden), f32),
            pltpu.VMEM((depth_s, right_extent * hidden), bf16),
            pltpu.VMEM((n_col, depth_s, width), bf16),
            pltpu.VMEM((n_row, depth_s, width), bf16),
            dma((n_col,)), dma((n_col,)),
            dma((n_row,)), dma((n_row,)),
            dma((n_col,)), dma((n_col,)),
            dma((n_row,)), dma((n_row,)),
            dma((n_col,)), dma((n_col,)),
            dma((n_row,)), dma((n_row,)),
            dma((n_col,)), dma((n_col,)),
        ],
        compiler_params=pltpu.CompilerParams(
            collective_id=0, has_side_effects=True, vmem_limit_bytes=56 * 1024 * 1024
        ),
    )(
        homolog_trait_tensor,
        gain,
        projections,
        result_matrix,
        result_offset[None, :],
        depth_lanes,
        recip,
        upstream_adjoint.reshape(left_extent * right_extent, pair_width),
    )
    return update.reshape(left_extent, right_extent, pair_width), slope, grad_w


def solution(mesh):
    in_specs = (P(None, ("row", "col")), P(), P(), P(), P(), P(), P(), P(), P("row", "col", None))
    out_specs = (P("row", "col", None), P(None, ("row", "col")), P())
    return jax.shard_map(body, mesh=mesh, in_specs=in_specs, out_specs=out_specs, check_vma=False)
```

time: 248 us -> 71.5 us (0.29)
  the two profiles are of different devices: /device:TPU:1 before, /device:TPU:24 now
where the time goes in v1:
time: 71.5 us; the launch traced here: 71.2 us
  Pallas kernels  61.9 us (87%)
  local copies, waits for them, and re-layouts  6.97 us (10%)
  other arithmetic  1.65 us (2%)
    pallas_call x1, Pallas kernels, body(): pl.pallas_call(functools.partial(kernel, n_row, n_col, hidden, embed), ou...  61.9 us
    unnamed x15, local copies, waits for them, and re-layouts  4.7 us

profile of v1, /device:TPU:24, one launch (start us, length us, event | category | flops | bytes accessed | tf_op | source)
XLA Modules:
  0.0 71.2 jit_solution(6058163449595533176)
XLA Ops:
  0.6 0.0 copy-start.4
  0.7 0.0 copy-start.5
  0.7 0.6 copy-done.4
  1.3 0.0 copy-done.5
  1.3 0.1 select_reduce_fusion
  1.4 0.1 dynamic_slice.11
  1.5 0.1 dynamic_slice.10
  1.6 0.1 dynamic_slice.9
  1.6 0.1 broadcast_in_dim.34
  1.7 0.0 copy-start.3
  1.7 0.7 broadcast_in_dim_reshape.4.depth_ref
  2.4 0.0 copy-done.3
  2.4 0.6 broadcast_in_dim_tile.3.gain_ref
  3.0 0.1 broadcast_in_dim.35
  3.1 0.1 min.16
  3.2 0.0 copy-start.1
  3.2 0.0 copy-start.2
  3.2 0.7 %add_divide_fusion.recip_ref = f32[32,512]{1,0:T(8,128)} fusion(s32[512]{0:T(512)S(1)} %min.16, s32[32]{0:T(128)S(1)} %dynamic_slice.10), kind=kLoop, calls=%fused_computation.1 | loop fusion | flops 65536 | bytes 67712 | tf_op jit(solution)/shard_map/div | solution.py:424
  3.9 0.0 copy-done.1
  3.9 0.0 copy-done.2
  3.9 0.2 broadcast_multiply_fusion.1
  4.1 0.1 mul.56
  4.2 0.1 copy.16
  4.3 0.1 mul.59
  4.5 0.1 copy.17
  4.6 0.7 pad_maximum_fusion.proj_ref
  5.3 61.9 %shard_map.112 = (bf16[512,128]{1,0:T(8,128)(2,1)}, f32[192,256]{1,0:T(8,128)}, f32[1024,128]{1,0:T(8,128)}) custom-call(bf16[192,256]{1,0:T(8,128)(2,1)} %x_ref.1, f32[1,256]{1,0:T(1,128)} %broadcast_in_dim_tile.3.gain_ref, bf16[256,256]{1,0:T(8,128)(2,1)} %pad_maximum_fusion.proj_ref, bf16[1024,128]{1,0:T(8,128)(2,1)} %w_ref.1, f32[1,128]{1,0:T(1,128)} %bitcast.9, ...), custom_call_target="tpu_custom_call" | custom-call | tf_op jit(solution)/shard_map/pallas_call | solution.py:436
  67.1 0.0 copy-start
  67.2 1.6 %copy.21 = bf16[32,16,128]{2,1,0:T(8,128)(2,1)} copy(bf16[32,16,128]{2,1,0:T(8,128)(2,1)} %bitcast.7) | data formatting | bytes 262144
  68.8 1.6 %copy.22 = f32[192,256]{1,0:T(8,128)} copy(f32[192,256]{1,0:T(8,128)} %get-tuple-element.15) | data formatting | bytes 393216
  70.4 0.0 copy-done
  70.4 0.8 %copy.23 = f32[1024,128]{1,0:T(8,128)} copy(f32[1024,128]{1,0:T(8,128)S(1)} %copy-done) | data formatting | bytes 1048576
  (2 shorter events, 0.0 us)
Async XLA Ops:
  0.6 0.7 copy-start.4
  0.7 0.7 copy-start.5
  1.7 0.7 copy-start.3
  3.2 0.7 %copy-start.1 = (bf16[64,32]{0,1:T(8,128)(2,1)S(1)}, bf16[64,32]{0,1:T(8,128)(2,1)}, u32[]{:S(2)}) copy-start(bf16[64,32]{0,1:T(8,128)(2,1)} %param.11) | copy-start | bytes 12292
  3.2 0.7 %copy-start.2 = (bf16[64,32]{0,1:T(8,128)(2,1)S(1)}, bf16[64,32]{0,1:T(8,128)(2,1)}, u32[]{:S(2)}) copy-start(bf16[64,32]{0,1:T(8,128)(2,1)} %param.12) | copy-start | bytes 12292
  67.1 3.3 %copy-start = (f32[1024,128]{1,0:T(8,128)S(1)}, f32[1024,128]{1,0:T(8,128)}, u32[]{:S(2)}) copy-start(f32[1024,128]{1,0:T(8,128)} %get-tuple-element.16) | copy-start | bytes 1572868

commit v2 on v1

--- a/solution.py
+++ b/solution.py
@@ -38,10 +38,12 @@
     x_ref, gain_ref, proj_ref, w_ref, offset_ref, depth_ref, recip_ref, adj_ref,
     upd_ref, slope_ref, gw_out_ref,
     normed_ref, inv_ref, lsend_ref, rsend_ref, lall_ref, rall_ref, prod_ref, flat_ref,
-    adjf_ref, adjt_ref, updf_ref, gacc_ref, gwsend_ref, w1_ref, w2_ref, w3_ref,
-    go_ref, gm_ref, glsend_ref, gracc_ref, grsend_ref, gl_ref, gr_ref,
-    ls_sem, lr_sem, rs_sem, rr_sem, gls_sem, glr_sem, grs_sem, grr_sem,
-    w1s_sem, w1r_sem, w2s_sem, w2r_sem, w3s_sem, w3r_sem,
+    adjf_ref, adjt_ref, updf_ref, gacc_ref, gwsend_ref, w1_ref, w2send_ref, w2_ref, w4_ref,
+    go_ref, gm_ref, glsend_ref, glp_ref, glsum_ref, gl_ref,
+    gracc_ref, grsend_ref, gr_ref, grsum_ref, grfin_ref,
+    ls_sem, lf_sem, lr_sem, rs_sem, rr_sem, gps_sem, gpr_sem, gls_sem, glr_sem,
+    grs_sem, grr_sem, hop_sem, w1s_sem, w1r_sem, w2s_sem, w2r_sem, w3s_sem, w3r_sem,
+    w4s_sem, w4r_sem,
 ):
     r = lax.axis_index("row")
     c = lax.axis_index("col")
@@ -59,7 +61,10 @@
     to_slot = lax.rem(c, n_row)
     own_row = c // group
     own_col = lax.rem(c, group) * n_row
-    loops_back = to_col == c
+    fixed = (to_col == c) & (to_slot == r)
+    half = n_col // 2
+    pair, side = c // 2, lax.rem(c, 2)
+    partner = c + 1 - 2 * side
 
     barrier = pltpu.get_barrier_semaphore()
 
@@ -72,17 +77,11 @@
         greet(r, lax.rem(c + o, n_col))
     for o in range(1, n_row):
         greet(lax.rem(r + o, n_row), c)
-    for k in range(n_row):
-        self_target = loops_back & (r == k)
-        self_owner = (own_row == r) & (own_col + k == c)
-
-        @pl.when(jnp.logical_not(self_target))
-        def _():
-            greet(k, to_col)
-
-        @pl.when(jnp.logical_not(self_owner))
-        def _():
-            greet(own_row, own_col + k)
+
+    @pl.when(jnp.logical_not(fixed))
+    def _():
+        greet(to_slot, to_col)
+        greet(own_row, own_col + r)
 
     def remote(src, dst, send_sem, recv_sem, row, col):
         return pltpu.make_async_remote_copy(
@@ -116,33 +115,50 @@
         return ref.at[:, pl.ds(pl.multiple_of(index * width, LANES), width)]
 
     pl.semaphore_wait(
-        barrier, n_col - 1 + n_row - 1 + 2 * n_row - 2 * loops_back.astype(jnp.int32)
+        barrier, n_col - 1 + n_row - 1 + 2 - 2 * fixed.astype(jnp.int32)
     )
 
+    def same_side(o):
+        return lax.rem(pair + o, half) * 2 + side
+
+    def right_hop():
+        return remote(
+            rsend_ref, panel(rall_ref, to_slot), hop_sem.at[0], rr_sem.at[to_slot],
+            to_slot, to_col,
+        )
+
+    def right_copy(o):
+        return remote(
+            panel(rall_ref, r), panel(rall_ref, r), rs_sem.at[o], rr_sem.at[r],
+            lax.rem(r + o, n_row), c,
+        )
+
     def left_copy(o):
-        return remote(
-            lsend_ref, panel(lall_ref, c), ls_sem.at[o], lr_sem.at[c],
-            r, lax.rem(c + o, n_col),
-        )
-
-    def right_copy(k):
-        return remote(
-            rsend_ref, panel(rall_ref, to_slot), rs_sem.at[k], rr_sem.at[to_slot], k, to_col
-        )
-
-    for k in range(n_row):
-        self_target = loops_back & (r == k)
-
-        @pl.when(jnp.logical_not(self_target))
-        def _():
-            right_copy(k).start()
-
-    for o in range(1, n_col):
+        target = partner if o == 0 else same_side(o)
+        return remote(lsend_ref, panel(lall_ref, c), ls_sem.at[o], lr_sem.at[c], r, target)
+
+    def left_relay(o):
+        source = same_side(half - o)
+        return remote(
+            panel(lall_ref, source), panel(lall_ref, source), lf_sem.at[o], lr_sem.at[source],
+            r, partner,
+        )
+
+    def left_arrival(source):
+        remote(
+            lsend_ref, panel(lall_ref, source), ls_sem.at[0], lr_sem.at[source], r, partner
+        ).wait_recv()
+
+    @pl.when(jnp.logical_not(fixed))
+    def _():
+        right_hop().start()
+
+    @pl.when(fixed)
+    def _():
+        panel(rall_ref, r)[...] = rsend_ref[...]
+
+    for o in range(half):
         left_copy(o).start()
-
-    @pl.when(loops_back & (r == own_row))
-    def _():
-        panel(rall_ref, to_slot)[...] = rsend_ref[...]
 
     panel(lall_ref, c)[...] = left
 
@@ -154,20 +170,25 @@
                 pl.ds(j, BLOCK, stride=right_extent), :
             ].astype(bf16)
 
-    for k in range(n_row):
-        self_owner = (own_row == r) & (own_col + k == c)
-
-        @pl.when(jnp.logical_not(self_owner))
-        def _():
-            remote(
-                rsend_ref, panel(rall_ref, k), rs_sem.at[k], rr_sem.at[k], own_row, own_col + k
-            ).wait_recv()
-
-    for o in range(1, n_col):
-        source = lax.rem(c + o, n_col)
-        remote(
-            lsend_ref, panel(lall_ref, source), ls_sem.at[o], lr_sem.at[source], r, source
-        ).wait_recv()
+    def right_arrival(slot):
+        remote(
+            rsend_ref, panel(rall_ref, slot), hop_sem.at[0], rr_sem.at[slot],
+            to_slot, to_col,
+        ).wait_recv()
+
+    @pl.when(jnp.logical_not(fixed))
+    def _():
+        right_arrival(r)
+
+    for o in range(1, n_row):
+        right_copy(o).start()
+    for o in range(1, half):
+        left_arrival(same_side(half - o))
+        left_relay(o).start()
+    for o in range(1, n_row):
+        right_arrival(lax.rem(r + o, n_row))
+    for o in range(half):
+        left_arrival(lax.rem(pair + o, half) * 2 + 1 - side)
 
     lane_part = lax.broadcasted_iota(jnp.int32, (BLOCK, LANES), 1) // hidden
     groups_j = right_extent // per_vreg
@@ -216,21 +237,19 @@
 
     lax.fori_loop(0, chunks, forward, 0)
 
-    piece = channels // n_col
-    gwsend_ref[...] = gacc_ref[...].T.astype(bf16)
-
-    def w_rows(ref, index):
-        return ref.at[pl.ds(pl.multiple_of(index * piece, piece), piece), :]
+    part = channels // n_row
+    piece = part // n_col
+    gwsend_ref[...] = gacc_ref[...].T.reshape(n_row, part, gacc_ref.shape[0]).astype(bf16)
 
     def w1_copy(o):
-        target = lax.rem(c + o, n_col)
-        return remote(
-            w_rows(gwsend_ref, target), w1_ref.at[c], w1s_sem.at[o], w1r_sem.at[c], r, target
-        )
-
-    for o in range(1, n_col):
+        target = lax.rem(r + o, n_row)
+        return remote(
+            gwsend_ref.at[target], w1_ref.at[r], w1s_sem.at[o], w1r_sem.at[r], target, c
+        )
+
+    for o in range(1, n_row):
         w1_copy(o).start()
-    w1_ref[c] = w_rows(gwsend_ref, c)[...]
+    w1_ref[r] = gwsend_ref[r]
 
     gracc_ref[...] = jnp.zeros_like(gracc_ref)
 
@@ -262,92 +281,137 @@
 
     lax.fori_loop(0, chunks, backward, 0)
 
+    def gp_copy(o):
+        q = lax.rem(pair + o, half)
+        return remote(
+            panel(glsend_ref, q * 2 + 1 - side), glp_ref.at[q], gps_sem.at[o], gpr_sem.at[q],
+            r, partner,
+        )
+
     def gl_copy(o):
+        q = lax.rem(pair + o, half)
+        return remote(
+            glsum_ref.at[q], gl_ref.at[pair], gls_sem.at[o], glr_sem.at[pair], r, q * 2 + side
+        )
+
+    def gr_copy(o):
+        target = lax.rem(r + o, n_row)
+        return remote(
+            panel(grsend_ref, target), gr_ref.at[r], grs_sem.at[o], grr_sem.at[r], target, c
+        )
+
+    def gr_hop():
+        return remote(
+            grsum_ref, grfin_ref, hop_sem.at[1], hop_sem.at[2], own_row, own_col + r
+        )
+
+    def w2_copy(o):
         target = lax.rem(c + o, n_col)
         return remote(
-            panel(glsend_ref, target), gl_ref.at[c], gls_sem.at[o], glr_sem.at[c], r, target
-        )
-
-    def gr_copy(k):
-        return remote(
-            panel(grsend_ref, k), gr_ref.at[r], grs_sem.at[k], grr_sem.at[r],
-            own_row, own_col + k,
-        )
-
+            w2send_ref.at[target], w2_ref.at[c], w2s_sem.at[o], w2r_sem.at[c], r, target
+        )
+
+    def w3_copy(o):
+        return remote(
+            w4_ref.at[r, c], w4_ref.at[r, c], w3s_sem.at[o], w3r_sem.at[c],
+            r, lax.rem(c + o, n_col),
+        )
+
+    def w4_copy(o):
+        return remote(
+            w4_ref.at[r], w4_ref.at[r], w4s_sem.at[o], w4r_sem.at[r], lax.rem(r + o, n_row), c
+        )
+
+    for step in range(1, half + 1):
+        gp_copy(step % half).start()
+    grsend_ref[...] = gracc_ref[...].astype(bf16)
+    for o in range(1, n_row):
+        gr_copy(o).start()
+    gr_ref[r] = panel(grsend_ref, r)[...]
+
+    for o in range(1, n_row):
+        source = lax.rem(r + o, n_row)
+        remote(
+            gwsend_ref.at[source], w1_ref.at[source], w1s_sem.at[o], w1r_sem.at[source],
+            source, c,
+        ).wait_recv()
+    partial = w1_ref[0].astype(f32)
+    for d in range(1, n_row):
+        partial = partial + w1_ref[d].astype(f32)
+    w2send_ref[...] = partial.reshape(n_col, piece, partial.shape[1]).astype(bf16)
+    w2_ref[c] = w2send_ref[c]
     for o in range(1, n_col):
-        gl_copy(o).start()
-    grsend_ref[...] = gracc_ref[...].astype(bf16)
-    gl_ref[c] = panel(glsend_ref, c)[...]
-    for k in range(n_row):
-        self_owner = (own_row == r) & (own_col + k == c)
-
-        @pl.when(jnp.logical_not(self_owner))
-        def _():
-            gr_copy(k).start()
-
-        @pl.when(self_owner)
-        def _():
-            gr_ref[r] = panel(grsend_ref, k)[...]
-
-    for o in range(1, n_col):
-        source = lax.rem(c + o, n_col)
-        remote(
-            w_rows(gwsend_ref, source), w1_ref.at[source], w1s_sem.at[o], w1r_sem.at[source],
-            r, source,
-        ).wait_recv()
-    partial = w1_ref[0].astype(f32)
-    for d in range(1, n_col):
-        partial = partial + w1_ref[d].astype(f32)
-    w2_ref[r] = partial.astype(bf16)
-
-    def w2_copy(o):
-        return remote(
-            w2_ref.at[r], w2_ref.at[r], w2s_sem.at[o], w2r_sem.at[r], lax.rem(r + o, n_row), c
-        )
-
-    for o in range(1, n_row):
         w2_copy(o).start()
 
+    for step in range(1, half + 1):
+        o = step % half
+        q = lax.rem(pair + o, half)
+        remote(
+            panel(glsend_ref, 0), glp_ref.at[q], gps_sem.at[o], gpr_sem.at[q], r, partner
+        ).wait_recv()
+        joint = panel(glsend_ref, q * 2 + side)[...].astype(f32) + glp_ref[q].astype(f32)
+        if o:
+            glsum_ref[q] = joint.astype(bf16)
+            gl_copy(o).start()
+        else:
+            gl_ref[pair] = joint.astype(bf16)
+
     for o in range(1, n_row):
         source = lax.rem(r + o, n_row)
         remote(
-            w2_ref.at[source], w2_ref.at[source], w2s_sem.at[o], w2r_sem.at[source], source, c
-        ).wait_recv()
-    whole = w2_ref[0].astype(f32)
-    for d in range(1, n_row):
-        whole = whole + w2_ref[d].astype(f32)
-    w_rows(w3_ref, c)[...] = (whole * (1.0 / total)).astype(bf16)
-
-    def w3_copy(o):
-        return remote(
-            w_rows(w3_ref, c), w_rows(w3_ref, c), w3s_sem.at[o], w3r_sem.at[c],
-            r, lax.rem(c + o, n_col),
-        )
-
-    for o in range(1, n_col):
-        w3_copy(o).start()
-
-    for o in range(1, n_col):
-        source = lax.rem(c + o, n_col)
-        remote(
-            panel(glsend_ref, source), gl_ref.at[source], gls_sem.at[o], glr_sem.at[source],
-            r, source,
-        ).wait_recv()
-    for k in range(n_row):
-        self_target = loops_back & (r == k)
-
-        @pl.when(jnp.logical_not(self_target))
-        def _():
-            remote(
-                panel(grsend_ref, 0), gr_ref.at[k], grs_sem.at[k], grr_sem.at[k], k, to_col
-            ).wait_recv()
-
-    grad_left = gl_ref[0].astype(f32)
-    for d in range(1, n_col):
-        grad_left = grad_left + gl_ref[d].astype(f32)
+            panel(grsend_ref, source), gr_ref.at[source], grs_sem.at[o], grr_sem.at[source],
+            source, c,
+        ).wait_recv()
     grad_right = gr_ref[0].astype(f32)
     for d in range(1, n_row):
         grad_right = grad_right + gr_ref[d].astype(f32)
+    grsum_ref[...] = grad_right.astype(bf16)
+
+    @pl.when(jnp.logical_not(fixed))
+    def _():
+        gr_hop().start()
+
+    @pl.when(fixed)
+    def _():
+        grfin_ref[...] = grsum_ref[...]
+
+    for o in range(1, n_col):
+        source = lax.rem(c + o, n_col)
+        remote(
+            w2send_ref.at[source], w2_ref.at[source], w2s_sem.at[o], w2r_sem.at[source],
+            r, source,
+        ).wait_recv()
+    whole = w2_ref[0].astype(f32)
+    for d in range(1, n_col):
+        whole = whole + w2_ref[d].astype(f32)
+    w4_ref[r, c] = (whole * (1.0 / total)).astype(bf16)
+    for o in range(1, n_col):
+        w3_copy(o).start()
+
+    for o in range(1, half):
+        source = lax.rem(pair + o, half)
+        remote(
+            glsum_ref.at[source], gl_ref.at[source], gls_sem.at[o], glr_sem.at[source],
+            r, source * 2 + side,
+        ).wait_recv()
+
+    @pl.when(jnp.logical_not(fixed))
+    def _():
+        gr_hop().wait_recv()
+
+    for o in range(1, n_col):
+        source = lax.rem(c + o, n_col)
+        remote(
+            w4_ref.at[r, source], w4_ref.at[r, source], w3s_sem.at[o], w3r_sem.at[source],
+            r, source,
+        ).wait_recv()
+    for o in range(1, n_row):
+        w4_copy(o).start()
+
+    grad_left = gl_ref[0].astype(f32)
+    for d in range(1, half):
+        grad_left = grad_left + gl_ref[d].astype(f32)
+    grad_right = grfin_ref[...].astype(f32)
     keep = (
         lax.broadcasted_iota(jnp.int32, (depth_s, width), 0) < depth_ref[...]
     ).astype(f32)
@@ -360,32 +424,32 @@
         - normed * dot_exact(grad_norm * normed, averager, NN)
     )
 
+    for o in range(1, n_row):
+        source = lax.rem(r + o, n_row)
+        remote(
+            w4_ref.at[source], w4_ref.at[source], w4s_sem.at[o], w4r_sem.at[source], source, c
+        ).wait_recv()
+    gw_out_ref[...] = w4_ref[...].astype(f32).reshape(gw_out_ref.shape)
+
+    for o in range(half):
+        left_copy(o).wait_send()
+        gp_copy(o).wait_send()
+    for o in range(1, half):
+        left_relay(o).wait_send()
+        gl_copy(o).wait_send()
     for o in range(1, n_col):
-        source = lax.rem(c + o, n_col)
-        remote(
-            w_rows(w3_ref, source), w_rows(w3_ref, source), w3s_sem.at[o], w3r_sem.at[source],
-            r, source,
-        ).wait_recv()
-    gw_out_ref[...] = w3_ref[...].astype(f32)
-
-    for o in range(1, n_col):
-        left_copy(o).wait_send()
+        w2_copy(o).wait_send()
+        w3_copy(o).wait_send()
+    for o in range(1, n_row):
+        right_copy(o).wait_send()
+        gr_copy(o).wait_send()
         w1_copy(o).wait_send()
-        gl_copy(o).wait_send()
-        w3_copy(o).wait_send()
-    for o in range(1, n_row):
-        w2_copy(o).wait_send()
-    for k in range(n_row):
-        self_target = loops_back & (r == k)
-        self_owner = (own_row == r) & (own_col + k == c)
-
-        @pl.when(jnp.logical_not(self_target))
-        def _():
-            right_copy(k).wait_send()
-
-        @pl.when(jnp.logical_not(self_owner))
-        def _():
-            gr_copy(k).wait_send()
+        w4_copy(o).wait_send()
+
+    @pl.when(jnp.logical_not(fixed))
+    def _():
+        right_hop().wait_send()
+        gr_hop().wait_send()
 
 
 def body(
@@ -414,6 +478,8 @@
     channels = hidden * hidden
     rows = BLOCK * right_extent
     span = BLOCK * hidden
+    half = n_col // 2
+    piece = channels // (n_row * n_col)
 
     table = position_molecule[:, None] == jnp.arange(sequence_tallies.shape[0])[None, :]
     depth = jnp.sum(jnp.where(table, sequence_tallies[None, :], 0), axis=1)
@@ -455,24 +521,28 @@
             pltpu.VMEM((left_extent * right_extent, pair_width), bf16),
             pltpu.VMEM((rows, pair_width), f32),
             pltpu.VMEM((pair_width, channels), f32),
-            pltpu.VMEM((channels, pair_width), bf16),
-            pltpu.VMEM((n_col, channels // n_col, pair_width), bf16),
-            pltpu.VMEM((n_row, channels // n_col, pair_width), bf16),
-            pltpu.VMEM((channels, pair_width), bf16),
+            pltpu.VMEM((n_row, channels // n_row, pair_width), bf16),
+            pltpu.VMEM((n_row, channels // n_row, pair_width), bf16),
+            pltpu.VMEM((n_col, piece, pair_width), bf16),
+            pltpu.VMEM((n_col, piece, pair_width), bf16),
+            pltpu.VMEM((n_row, n_col, piece, pair_width), bf16),
             pltpu.VMEM((rows, channels), f32),
             pltpu.VMEM((right_extent * hidden // LANES, span, LANES), f32),
             pltpu.VMEM((depth_s, left_extent * hidden), bf16),
+            pltpu.VMEM((half, depth_s, width), bf16),
+            pltpu.VMEM((half, depth_s, width), bf16),
+            pltpu.VMEM((half, depth_s, width), bf16),
             pltpu.VMEM((depth_s, right_extent * hidden), f32),
             pltpu.VMEM((depth_s, right_extent * hidden), bf16),
-            pltpu.VMEM((n_col, depth_s, width), bf16),
             pltpu.VMEM((n_row, depth_s, width), bf16),
-            dma((n_col,)), dma((n_col,)),
+            pltpu.VMEM((depth_s, width), bf16),
+            pltpu.VMEM((depth_s, width), bf16),
+            dma((half,)), dma((half,)), dma((n_col,)),
             dma((n_row,)), dma((n_row,)),
-            dma((n_col,)), dma((n_col,)),
-            dma((n_row,)), dma((n_row,)),
-            dma((n_col,)), dma((n_col,)),
-            dma((n_row,)), dma((n_row,)),
-            dma((n_col,)), dma((n_col,)),
+            dma((half,)), dma((half,)), dma((half,)), dma((half,)),
+            dma((n_row,)), dma((n_row,)), dma((3,)),
+            dma((n_row,)), dma((n_row,)), dma((n_col,)), dma((n_col,)),
+            dma((n_col,)), dma((n_col,)), dma((n_row,)), dma((n_row,)),
         ],
         compiler_params=pltpu.CompilerParams(
             collective_id=0, has_side_effects=True, vmem_limit_bytes=56 * 1024 * 1024

time: 71.5 us -> 52 us (0.73)
  the two profiles are of different devices: /device:TPU:24 before, /device:TPU:1 now
where the time goes in v2:
time: 52 us; the launch traced here: 51.7 us
  Pallas kernels  42.4 us (82%)
  local copies, waits for them, and re-layouts  6.97 us (13%)
  other arithmetic  1.65 us (3%)
  between operations  0.71 us (1%)
    pallas_call x1, Pallas kernels, body(): pl.pallas_call(functools.partial(kernel, n_row, n_col, hidden, embed), ou...  42.4 us
    unnamed x15, local copies, waits for them, and re-layouts  4.7 us

profile of v2, /device:TPU:1, one launch (start us, length us, event | category | flops | bytes accessed | tf_op | source)
XLA Modules:
  0.0 51.7 jit_solution(17435425913707050611)
XLA Ops:
  0.6 0.0 copy-start.4
  0.7 0.0 copy-start.5
  0.7 0.6 %copy-done.4 = s32[16]{0:T(128)S(1)} copy-done((s32[16]{0:T(128)S(1)}, s32[16]{0:T(128)}, u32[]{:S(2)}) %copy-start.4) | copy-done | bytes 88
  1.3 0.0 copy-done.5
  1.3 0.1 select_reduce_fusion
  1.4 0.1 dynamic_slice.11
  1.5 0.1 dynamic_slice.10
  1.6 0.1 dynamic_slice.9
  1.6 0.1 broadcast_in_dim.34
  1.7 0.0 copy-start.3
  1.7 0.7 %broadcast_in_dim_reshape.4.depth_ref = s32[1,128]{1,0:T(1,128)} reshape(s32[4,32]{1,0:T(4,128)S(1)} %broadcast_in_dim.34) | data formatting | bytes 1024 | tf_op jit(solution)/shard_map/broadcast_in_dim;reshape | solution.py:489
  2.4 0.0 copy-done.3
  2.4 0.6 %broadcast_in_dim_tile.3.gain_ref = f32[1,256]{1,0:T(1,128)} reshape(f32[4,64]{1,0:T(4,128)S(1)} %tile.2) | data formatting | bytes 2048 | tf_op jit(solution)/shard_map/broadcast_in_dim;tile | solution.py:498
  3.0 0.1 broadcast_in_dim.35
  3.1 0.1 min.16
  3.2 0.0 copy-start.1
  3.2 0.0 copy-start.2
  3.2 0.7 %add_divide_fusion.recip_ref = f32[32,512]{1,0:T(8,128)} fusion(s32[512]{0:T(512)S(1)} %min.16, s32[32]{0:T(128)S(1)} %dynamic_slice.10), kind=kLoop, calls=%fused_computation.1 | loop fusion | flops 65536 | bytes 67712 | tf_op jit(solution)/shard_map/div | solution.py:490
  3.9 0.0 copy-done.1
  3.9 0.0 copy-done.2
  3.9 0.2 broadcast_multiply_fusion.1
  4.1 0.1 mul.56
  4.2 0.1 copy.16
  4.3 0.1 mul.59
  4.5 0.1 copy.17
  4.6 0.7 %pad_maximum_fusion.proj_ref = bf16[256,256]{1,0:T(8,128)(2,1)} fusion(bf16[256,128]{1,0:T(8,128)(2,1)S(1)} %copy.17, bf16[256,128]{1,0:T(8,128)(2,1)S(1)} %copy.16), kind=kLoop, calls=%fused_computation | loop fusion | flops 262144 | bytes 262144 | tf_op jit(solution)/shard_map/concatenate | solution.py:495
  5.3 42.4 %shard_map.112 = (bf16[512,128]{1,0:T(8,128)(2,1)}, f32[192,256]{1,0:T(8,128)}, f32[1024,128]{1,0:T(8,128)}) custom-call(bf16[192,256]{1,0:T(8,128)(2,1)} %x_ref.1, f32[1,256]{1,0:T(1,128)} %broadcast_in_dim_tile.3.gain_ref, bf16[256,256]{1,0:T(8,128)(2,1)} %pad_maximum_fusion.proj_ref, bf16[1024,128]{1,0:T(8,128)(2,1)} %w_ref.1, f32[1,128]{1,0:T(1,128)} %bitcast.9, ...), custom_call_target="tpu_custom_call" | custom-call | tf_op jit(solution)/shard_map/pallas_call | solution.py:502
  47.7 0.0 copy-start
  47.7 1.6 %copy.21 = bf16[32,16,128]{2,1,0:T(8,128)(2,1)} copy(bf16[32,16,128]{2,1,0:T(8,128)(2,1)} %bitcast.7) | data formatting | bytes 262144
  49.3 1.6 %copy.22 = f32[192,256]{1,0:T(8,128)} copy(f32[192,256]{1,0:T(8,128)} %get-tuple-element.15) | data formatting | bytes 393216
  50.9 0.0 copy-done
  50.9 0.8 %copy.23 = f32[1024,128]{1,0:T(8,128)} copy(f32[1024,128]{1,0:T(8,128)S(1)} %copy-done) | data formatting | bytes 1048576
  (2 shorter events, 0.0 us)
Async XLA Ops:
  0.6 0.7 %copy-start.4 = (s32[16]{0:T(128)S(1)}, s32[16]{0:T(128)}, u32[]{:S(2)}) copy-start(s32[16]{0:T(128)} %param.15) | copy-start | bytes 196
  0.7 0.7 %copy-start.5 = (s32[128]{0:T(128)S(1)}, s32[128]{0:T(128)}, u32[]{:S(2)}) copy-start(s32[128]{0:T(128)} %param.16) | copy-start | bytes 1540
  1.7 0.7 %copy-start.3 = (f32[64]{0:T(128)S(1)}, f32[64]{0:T(128)}, u32[]{:S(2)}) copy-start(f32[64]{0:T(128)} %param.10) | copy-start | bytes 772
  3.2 0.7 %copy-start.1 = (bf16[64,32]{0,1:T(8,128)(2,1)S(1)}, bf16[64,32]{0,1:T(8,128)(2,1)}, u32[]{:S(2)}) copy-start(bf16[64,32]{0,1:T(8,128)(2,1)} %param.11) | copy-start | bytes 12292
  3.2 0.7 %copy-start.2 = (bf16[64,32]{0,1:T(8,128)(2,1)S(1)}, bf16[64,32]{0,1:T(8,128)(2,1)}, u32[]{:S(2)}) copy-start(bf16[64,32]{0,1:T(8,128)(2,1)} %param.12) | copy-start | bytes 12292
  47.7 3.3 %copy-start = (f32[1024,128]{1,0:T(8,128)S(1)}, f32[1024,128]{1,0:T(8,128)}, u32[]{:S(2)}) copy-start(f32[1024,128]{1,0:T(8,128)} %get-tuple-element.16) | copy-start | bytes 1572868

commit v3 on v2

--- a/solution.py
+++ b/solution.py
@@ -35,7 +35,7 @@
 
 def kernel(
     n_row, n_col, hidden, embed,
-    x_ref, gain_ref, proj_ref, w_ref, offset_ref, depth_ref, recip_ref, adj_ref,
+    x_ref, gain_ref, proj_ref, w_ref, offset_ref, tallies_ref, position_ref, adj_ref,
     upd_ref, slope_ref, gw_out_ref,
     normed_ref, inv_ref, lsend_ref, rsend_ref, lall_ref, rall_ref, prod_ref, flat_ref,
     adjf_ref, adjt_ref, updf_ref, gacc_ref, gwsend_ref, w1_ref, w2send_ref, w2_ref, w4_ref,
@@ -43,7 +43,7 @@
     gracc_ref, grsend_ref, gr_ref, grsum_ref, grfin_ref,
     ls_sem, lf_sem, lr_sem, rs_sem, rr_sem, gps_sem, gpr_sem, gls_sem, glr_sem,
     grs_sem, grr_sem, hop_sem, w1s_sem, w1r_sem, w2s_sem, w2r_sem, w3s_sem, w3r_sem,
-    w4s_sem, w4r_sem,
+    w4s_sem, w4r_sem, recip_ref, keep_ref,
 ):
     r = lax.axis_index("row")
     c = lax.axis_index("col")
@@ -101,10 +101,21 @@
     normed = centred * inv
     normed_ref[...] = normed
     inv_ref[...] = inv
-    gain = gain_ref[...]
+    gain = jnp.concatenate([gain_ref[...]] * (full // embed), axis=1)
+
+    def spread(shape, axis, each, first, count):
+        place = lax.broadcasted_iota(jnp.int32, shape, axis) // each
+        depths = jnp.zeros(shape, jnp.int32)
+        for t in range(count):
+            depths = jnp.where(place == t, tallies_ref[position_ref[first + t]], depths)
+        return depths
+
+    local = full // embed
     keep = (
-        lax.broadcasted_iota(jnp.int32, (depth_s, width), 0) < depth_ref[...]
+        lax.broadcasted_iota(jnp.int32, (depth_s, width), 0)
+        < spread((1, width), 1, hidden, (r * n_col + c) * local, local)
     ).astype(f32)
+    keep_ref[...] = keep
     both = dot_exact(normed * gain, proj_ref[...], NN)
     left = (both[:, :width] * keep).astype(bf16)
     right = (both[:, width:] * keep).astype(bf16)
@@ -163,7 +174,13 @@
     panel(lall_ref, c)[...] = left
 
     rows = BLOCK * right_extent
+    over_cols = spread(
+        (1, recip_ref.shape[1]), 1, hidden, c * right_extent, right_extent
+    )
     for b in range(chunks):
+        over_rows = spread((BLOCK, 1), 0, 1, r * left_extent + b * BLOCK, BLOCK)
+        counts = jnp.minimum(over_rows, over_cols).astype(f32) + EPS_COUNT
+        recip_ref[b * BLOCK : (b + 1) * BLOCK, :] = 1.0 / counts
         adjf_ref[...] = adj_ref[b * rows : (b + 1) * rows, :].astype(f32)
         for j in range(right_extent):
             adjt_ref[b * rows + j * BLOCK : b * rows + (j + 1) * BLOCK, :] = adjf_ref[
@@ -412,11 +429,9 @@
     for d in range(1, half):
         grad_left = grad_left + gl_ref[d].astype(f32)
     grad_right = grfin_ref[...].astype(f32)
-    keep = (
-        lax.broadcasted_iota(jnp.int32, (depth_s, width), 0) < depth_ref[...]
-    ).astype(f32)
+    keep = keep_ref[...]
     sides = jnp.concatenate([grad_left * keep, grad_right * keep], axis=1)
-    grad_norm = dot_exact(sides, proj_ref[...], NT) * gain_ref[...]
+    grad_norm = dot_exact(sides, proj_ref[...], NT) * gain
     normed = normed_ref[...]
     slope_ref[...] = inv_ref[...] * (
         grad_norm
@@ -429,7 +444,7 @@
         remote(
             w4_ref.at[source], w4_ref.at[source], w4s_sem.at[o], w4r_sem.at[source], source, c
         ).wait_recv()
-    gw_out_ref[...] = w4_ref[...].astype(f32).reshape(gw_out_ref.shape)
+    gw_out_ref[...] = w4_ref[...].astype(f32).reshape(gw_out_ref.shape).astype(bf16)
 
     for o in range(half):
         left_copy(o).wait_send()
@@ -465,8 +480,6 @@
 ):
     n_row = lax.axis_size("row")
     n_col = lax.axis_size("col")
-    row_id = lax.axis_index("row")
-    col_id = lax.axis_index("col")
     depth_s, full = homolog_trait_tensor.shape
     embed, hidden = lefthand_projection.shape
     pair_width = result_matrix.shape[1]
@@ -481,32 +494,21 @@
     half = n_col // 2
     piece = channels // (n_row * n_col)
 
-    table = position_molecule[:, None] == jnp.arange(sequence_tallies.shape[0])[None, :]
-    depth = jnp.sum(jnp.where(table, sequence_tallies[None, :], 0), axis=1)
-    depth_local = lax.dynamic_slice_in_dim(depth, (row_id * n_col + col_id) * local, local)
-    depth_rows = lax.dynamic_slice_in_dim(depth, row_id * left_extent, left_extent)
-    depth_cols = lax.dynamic_slice_in_dim(depth, col_id * right_extent, right_extent)
-    depth_lanes = jnp.repeat(depth_local, hidden)[None, :]
-    recip = 1.0 / (
-        jnp.minimum(depth_rows[:, None], jnp.repeat(depth_cols, hidden)[None, :]).astype(f32)
-        + EPS_COUNT
-    )
     eye = jnp.eye(local, dtype=bf16)
     projections = jnp.concatenate(
         [jnp.kron(eye, lefthand_projection), jnp.kron(eye, righthand_projection)], axis=1
     )
-    gain = jnp.tile(whitening_multiplier, local)[None, :]
-
     vmem = pl.BlockSpec(memory_space=pltpu.VMEM)
+    smem = pl.BlockSpec(memory_space=pltpu.SMEM)
     dma = pltpu.SemaphoreType.DMA
     update, slope, grad_w = pl.pallas_call(
         functools.partial(kernel, n_row, n_col, hidden, embed),
         out_shape=(
             jax.ShapeDtypeStruct((left_extent * right_extent, pair_width), bf16),
             jax.ShapeDtypeStruct((depth_s, full), f32),
-            jax.ShapeDtypeStruct((channels, pair_width), f32),
+            jax.ShapeDtypeStruct((channels, pair_width), bf16),
         ),
-        in_specs=[vmem] * 8,
+        in_specs=[vmem] * 5 + [smem] * 2 + [vmem],
         out_specs=(vmem,) * 3,
         scratch_shapes=[
             pltpu.VMEM((depth_s, full), f32),
@@ -543,21 +545,23 @@
             dma((n_row,)), dma((n_row,)), dma((3,)),
             dma((n_row,)), dma((n_row,)), dma((n_col,)), dma((n_col,)),
             dma((n_col,)), dma((n_col,)), dma((n_row,)), dma((n_row,)),
+            pltpu.VMEM((left_extent, right_extent * hidden), f32),
+            pltpu.VMEM((depth_s, width), f32),
         ],
         compiler_params=pltpu.CompilerParams(
             collective_id=0, has_side_effects=True, vmem_limit_bytes=56 * 1024 * 1024
         ),
     )(
         homolog_trait_tensor,
-        gain,
+        whitening_multiplier[None, :],
         projections,
         result_matrix,
         result_offset[None, :],
-        depth_lanes,
-        recip,
+        sequence_tallies,
+        position_molecule,
         upstream_adjoint.reshape(left_extent * right_extent, pair_width),
     )
-    return update.reshape(left_extent, right_extent, pair_width), slope, grad_w
+    return update.reshape(left_extent, right_extent, pair_width), slope, grad_w.astype(f32)
 
 
 def solution(mesh):

time: 52 us -> 48.8 us (0.938)
  local copies, waits for them, and re-layouts: 6.97 us -> 2.17 us
  other arithmetic: 1.65 us -> 3.38 us
    unnamed x15 -> x6, local copies, waits for them, and re-layouts: 4.7 us -> 1.65 us
    convert_element_type x0 -> x1, other arithmetic: none -> 1.81 us  [body(): grad_w.astype(f32)]
    another operation x3 -> x0, local copies, waits for them, and re-layouts: 1.3 us -> none  [the longest x1 0.65 us: body(): depth_lanes = jnp.repeat(depth_local, hidden)[None, :]]
    div x1 -> x0, other arithmetic: 0.72 us -> none  [body(): 1.0 / (jnp.minimum(depth_rows[:, None], jnp.repeat(depth_cols, hidden)[No...]
    mul x1, other arithmetic: 0.16 us -> 0.88 us  [body(): jnp.kron(eye, lefthand_projection)]
where the time goes in v3:
time: 48.8 us; the launch traced here: 48.6 us
  Pallas kernels  42.3 us (87%)
  other arithmetic  3.38 us (7%)
  local copies, waits for them, and re-layouts  2.17 us (4%)
  between operations  0.68 us (1%)
    pallas_call x1, Pallas kernels, body(): pl.pallas_call(functools.partial(kernel, n_row, n_col, hidden, embed), ou...  42.3 us
    convert_element_type x1, other arithmetic, body(): grad_w.astype(f32)  1.81 us
    unnamed x6, local copies, waits for them, and re-layouts  1.65 us

profile of v3, /device:TPU:1, one launch (start us, length us, event | category | flops | bytes accessed | tf_op | source)
XLA Modules:
  0.0 48.6 jit_solution(4779039025713189865)
XLA Ops:
  0.6 0.9 %broadcast_multiply_fusion.1 = (bf16[4,64,4,32]{1,0,3,2:T(4,128)(2,1)S(1)}, bf16[4,64,4,32]{1,0,3,2:T(4,128)(2,1)S(1)}) fusion(bf16[64,32]{0,1:T(8,128)(2,1)} %param.11, bf16[4,4]{0,1:T(4,128)(2,1)S(1)} %fusion, bf16[64,32]{0,1:T(8,128)(2,1)} %param.12), kind=kLoop, calls=%fused_computation.2 | loop fusion | flops 65536 | bytes 139296 | tf_op jit(solution)/shard_map/jit(kron)/mul | solution.py:499
  1.5 0.1 mul.44
  1.7 0.1 copy.14
  1.8 0.1 mul.47
  1.9 0.1 copy.15
  2.1 0.7 %pad_maximum_fusion.proj_ref = bf16[256,256]{1,0:T(8,128)(2,1)} fusion(bf16[256,128]{1,0:T(8,128)(2,1)S(1)} %copy.15, bf16[256,128]{1,0:T(8,128)(2,1)S(1)} %copy.14), kind=kLoop, calls=%fused_computation | loop fusion | flops 262144 | bytes 262144 | tf_op jit(solution)/shard_map/concatenate | solution.py:498
  2.7 42.3 %shard_map.112 = (bf16[512,128]{1,0:T(8,128)(2,1)}, f32[192,256]{1,0:T(8,128)}, bf16[1024,128]{1,0:T(8,128)(2,1)}) custom-call(bf16[192,256]{1,0:T(8,128)(2,1)} %x_ref.1, f32[1,64]{1,0:T(1,128)} %bitcast.10, bf16[256,256]{1,0:T(8,128)(2,1)} %pad_maximum_fusion.proj_ref, bf16[1024,128]{1,0:T(8,128)(2,1)} %w_ref.1, f32[1,128]{1,0:T(1,128)} %bitcast.11, ...), custom_call_target="tpu_custom_call" | custom-call | tf_op jit(solution)/shard_map/pallas_call | solution.py:504
  45.1 0.0 copy-start.1
  45.1 1.8 %convert_element_type.13 = f32[1024,128]{1,0:T(8,128)} convert(bf16[1024,128]{1,0:T(8,128)(2,1)} %get-tuple-element.8) | non-fusion elementwise | flops 131072 | bytes 786432 | tf_op jit(solution)/shard_map/convert_element_type | solution.py:564
  46.9 0.0 copy-done.1
  46.9 0.0 copy-start
  46.9 0.7 %copy.18 = bf16[32,16,128]{2,1,0:T(8,128)(2,1)} copy(bf16[32,16,128]{2,1,0:T(8,128)(2,1)S(1)} %bitcast.9) | data formatting | bytes 262144
  47.6 0.3 copy-done
  47.9 0.7 %copy.19 = f32[192,256]{1,0:T(8,128)} copy(f32[192,256]{1,0:T(8,128)S(1)} %copy-done) | data formatting | bytes 393216
  (1 shorter events, 0.0 us)
Async XLA Ops:
  45.1 1.8 %copy-start.1 = (bf16[512,128]{1,0:T(8,128)(2,1)S(1)}, bf16[512,128]{1,0:T(8,128)(2,1)}, u32[]{:S(2)}) copy-start(bf16[512,128]{1,0:T(8,128)(2,1)} %get-tuple-element.6) | copy-start | bytes 393220
  46.9 1.0 %copy-start = (f32[192,256]{1,0:T(8,128)S(1)}, f32[192,256]{1,0:T(8,128)}, u32[]{:S(2)}) copy-start(f32[192,256]{1,0:T(8,128)} %get-tuple-element.15) | copy-start | bytes 589828
